TPU v7x, 32 devices: a whole 2x2x4 slice. The times are simulated.
32 devices in a mesh: dp: 8 (over z, x), mp: 4 (over y, core).
Axes of the slice: x: 2, y: 2, z: 4, core: 2. Of those that a mesh axis runs over, the one named last changes fastest.
Arguments:
- acts: bfloat16 [2048, 4096], P('dp'), may hold values from -6 to 6
- cotangent: bfloat16 [2048, 2048], P('dp', 'mp'), may hold values from -0.13183594 to 0.13183594
- stats: float32 [4, 8, 2, 512, 512], P('mp', 'dp'), as said below
- owner_slot: int32 [8], replicated, may hold values from 0 to 7, as said below
Outputs:
- update: bfloat16 [8, 512, 2048], P(None, 'dp', 'mp')
- new_stats: float32 [4, 8, 2, 512, 512], P('mp', 'dp')
Inputs may be any that keep to these rules, and one draw needn't show every extreme that they name: Distinct slot numbers; row block w is held by device owner_slot[w] // 1 of dp at its position owner_slot[w] % 1; some device holds 1 block. Every stats[j, s, f] is a symmetric positive definite matrix.
All inputs are finite; a program needn't handle non-finite values.
Results may differ from a plain program's by a relative error of at most 0.012.
The roundings to bfloat16 on the way count: a program that leaves them out, or rounds other values in their place, can miss the bound.
Values may be sent and summed in bfloat16 or wider, within the bound.
A program may use at most 192 MiB of HBM per device.

v0:
```python
import jax
import jax.numpy as jnp
from jax import lax
from jax.sharding import PartitionSpec as P

ITERS = 5


BETA = 0.9
DAMPING = 0.001
EPSILON = 1e-06


def batched(former, latter):
    return jnp.einsum(
        "kij,kjl->kil",
        former.astype(jnp.bfloat16),
        latter.astype(jnp.bfloat16),
        preferred_element_type=jnp.float32,
    )


def inverse_roots(stat_pair):
    identity = jnp.eye(stat_pair.shape[-1], dtype=jnp.float32)
    damped = stat_pair + DAMPING * identity
    frob_norm = jnp.sqrt(jnp.sum(damped * damped, axis=(1, 2), keepdims=True) + EPSILON)
    moment = damped / frob_norm
    result = jnp.broadcast_to(identity, stat_pair.shape)
    for iteration in range(ITERS):
        factor = (5.0 * identity - moment) * 0.25
        if iteration == 0:
            result = factor
        else:
            result = batched(result, factor)
        if iteration + 1 < ITERS:
            square = batched(factor, factor)
            moment = batched(square, batched(square, moment))
    return result * frob_norm ** (-0.25)


def precondition(grad_block, stat_pair):
    gram_left = lax.dot_general(
        grad_block, grad_block, (((1,), (1,)), ((), ())), preferred_element_type=jnp.float32
    )
    gram_right = lax.dot_general(
        grad_block, grad_block, (((0,), (0,)), ((), ())), preferred_element_type=jnp.float32
    )
    new_pair = BETA * stat_pair + (1.0 - BETA) * jnp.stack([gram_left, gram_right])
    root_pair = inverse_roots(new_pair)
    left_applied = jnp.dot(
        root_pair[0].astype(jnp.bfloat16), grad_block, preferred_element_type=jnp.float32
    )
    direction = jnp.dot(
        left_applied.astype(jnp.bfloat16),
        root_pair[1].astype(jnp.bfloat16),
        preferred_element_type=jnp.float32,
    )
    grad_wide = grad_block.astype(jnp.float32)
    graft_ratio = jnp.sqrt(
        (jnp.mean(grad_wide * grad_wide) + EPSILON) / (jnp.mean(direction * direction) + EPSILON)
    )
    return ((direction * graft_ratio).astype(jnp.bfloat16), new_pair)


def keep_slot(grad_block, stat_pair):
    return (jnp.zeros_like(grad_block), stat_pair)


def on_device(acts, cotangent, stats, owner_slot):
    dp_count = lax.axis_size("dp")
    my_index = lax.axis_index("dp")
    blk_size = cotangent.shape[1]
    blocks = acts.shape[1] // blk_size
    slot_count = stats.shape[1]
    piece_rows = blk_size // dp_count
    split_acts = acts.reshape(acts.shape[0], blocks, blk_size)
    my_slots = my_index * slot_count + jnp.arange(slot_count, dtype=jnp.int32)
    holds_block = owner_slot[None, :] == my_slots[:, None]
    filled = jnp.any(holds_block, axis=1)
    my_rows = lax.psum_scatter(
        jnp.einsum("twr,tc->rwc", split_acts, cotangent, preferred_element_type=jnp.float32),
        "dp",
        scatter_dimension=0,
        tiled=True,
    ).astype(jnp.bfloat16)
    slot_ids = jnp.arange(dp_count * slot_count, dtype=jnp.int32)
    selector = (owner_slot[None, :] == slot_ids[:, None]).astype(jnp.bfloat16)
    outgoing = jnp.einsum(
        "sw,rwc->src", selector, my_rows, preferred_element_type=jnp.float32
    ).astype(jnp.bfloat16)
    outgoing = outgoing.reshape(dp_count, slot_count, piece_rows, blk_size)
    arrived = lax.all_to_all(outgoing, "dp", split_axis=0, concat_axis=2, tiled=True)
    owned_grads = arrived.reshape(slot_count, blk_size, blk_size)
    slot_update, slot_stats = lax.cond(
        filled[0], precondition, keep_slot, owned_grads[0], stats[0, 0]
    )
    update_list = [slot_update]
    stat_list = [slot_stats]
    updates = jnp.stack(update_list)
    new_stats = jnp.stack(stat_list)[None]
    outgoing_rows = updates.reshape(slot_count, dp_count, piece_rows, blk_size)
    returned = lax.all_to_all(outgoing_rows, "dp", split_axis=1, concat_axis=1, tiled=True)
    grid_ids = (
        jnp.arange(slot_count, dtype=jnp.int32)[:, None]
        + slot_count * jnp.arange(dp_count, dtype=jnp.int32)[None, :]
    )
    picker = (owner_slot[:, None, None] == grid_ids[None]).astype(jnp.bfloat16)
    result = jnp.einsum(
        "wsn,snrc->wrc", picker, returned, preferred_element_type=jnp.float32
    ).astype(jnp.bfloat16)
    return (result, new_stats)


def solution(mesh):
    return jax.shard_map(
        on_device,
        mesh=mesh,
        in_specs=(P("dp", None), P("dp", "mp"), P("mp", "dp", None, None, None), P()),
        out_specs=(P(None, "dp", "mp"), P("mp", "dp", None, None, None)),
        check_vma=False,
    )
```

profile of v0, /device:TPU:0, one launch (start us, length us, event | category | flops | bytes accessed | tf_op | source)
XLA Modules:
  0.0 265.3 jit_solution(8592918326225802116)
XLA Ops:
  7.2 3.2 %copy.27 = f32[1,1,2,512,512]{4,3,2,1,0:T(8,128)} copy(f32[1,1,2,512,512]{4,3,2,1,0:T(8,128)} %param.8) | data formatting | bytes 4194304
  11.4 3.5 %copy.11 = bf16[256,8,512]{0,1,2:T(8,128)(2,1)} copy(bf16[256,8,512]{2,1,0:T(8,128)(2,1)S(1)} %bitcast.62) | data formatting | bytes 4194304 | tf_op jit(solution)/shard_map/reshape | solution.py:76
  14.8 6.1 %convolution_bitcast_fusion.2 = f32[512,8,512]{2,1,0:T(8,128)} fusion(bf16[256,8,512]{0,1,2:T(8,128)(2,1)} %copy.11, bf16[256,512]{1,0:T(8,128)(2,1)S(1)} %copy-done), kind=kOutput, calls=%fused_computation.43 | convolution fusion | flops 1073741824 | bytes 10747904 | tf_op jit(solution)/shard_map/twr,tc->rwc/dot_general | solution.py:81
  20.9 150.3 %reduce-scatter.2.cloned.1.call-done = f32[64,8,512]{2,1,0:T(8,128)} async-done(((f32[512,8,512]{2,1,0:T(8,128)}), f32[64,8,512]{2,1,0:T(8,128)}) %reduce-scatter.2.cloned.1.call-update) | async-done | bytes 1048592 | tf_op jit(solution)/shard_map/reduce_scatter | solution.py:80
  171.3 1.5 fusion.16
  173.7 3.7 %all-to-all-start = ((bf16[8,1,64,512]{3,2,1,0:T(8,128)(2,1)}), bf16[8,1,64,512]{3,2,1,0:T(8,128)(2,1)S(1)}, u32[]{:S(2)}, u32[]{:S(2)}) async-start(bf16[8,1,64,512]{3,2,1,0:T(8,128)(2,1)} %copy.12), calls=%async_computation.1 | async-start | bytes 1048576 | tf_op jit(solution)/shard_map/all_to_all | solution.py:92
  178.9 13.2 %all-to-all-done = bf16[8,1,64,512]{3,2,1,0:T(8,128)(2,1)S(1)} async-done(((bf16[8,1,64,512]{3,2,1,0:T(8,128)(2,1)}), bf16[8,1,64,512]{3,2,1,0:T(8,128)(2,1)S(1)}, u32[]{:S(2)}, u32[]{:S(2)}) %all-to-all-start) | async-done | bytes 524320 | tf_op jit(solution)/shard_map/all_to_all | solution.py:92
  192.1 46.7 %conditional.1 = (bf16[512,512]{1,0:T(8,128)(2,1)}, f32[2,512,512]{2,1,0:T(8,128)}) conditional(s32[]{:T(128)} %convert_element_type.105, f32[2,512,512]{2,1,0:T(8,128)} %bitcast.65, (f32[2,512,512]{2,1,0:T(8,128)}, bf16[8,1,64,512]{3,2,1,0:T(8,128)(2,1)S(1)}) %tuple.32), branch_computations={%region_2.0_spmd, %region_3.0_spmd} | conditional | flops 9696444416 | bytes 114819456 | solution.py:94
  193.4 1.1 copy-done.5
  194.5 1.6 multiply_reduce_fusion
  196.1 1.3 copy-done.6
  197.4 2.2 convolution_convert_fusion.10
  199.6 3.8 %fusion.1 = f32[2,512,512]{2,1,0:T(8,128)S(1)} fusion(bf16[2,512,512]{2,1,0:T(8,128)(2,1)} %convolution_convert_fusion.10, f32[2,512,512]{2,1,0:T(8,128)} %copy-done.6, f32[2]{0:T(128)S(1)} %get-tuple-element.29, f32[512,512]{1,0:T(8,128)} %copy-done.7), kind=kOutput, calls=%fused_computation.21 | convolution fusion | flops 1075838976 | bytes 6291464 | tf_op jit(solution)/shard_map/cond/branch_1_fun/kij,kjl->kil/dot_general | solution.py:15
  203.4 1.3 copy-done.2
  204.8 1.7 convolution_convert_fusion.7
  206.5 3.5 %fusion.2 = f32[2,512,512]{2,1,0:T(8,128)S(1)} fusion(bf16[2,512,512]{2,1,0:T(8,128)(2,1)} %convolution_convert_fusion.7, f32[2,512,512]{2,1,0:T(8,128)} %copy-done.2), kind=kOutput, calls=%fused_computation.22 | convolution fusion | flops 1074790400 | bytes 5242880 | tf_op jit(solution)/shard_map/cond/branch_1_fun/kij,kjl->kil/dot_general | solution.py:15
  210.0 5.0 %convolution_convert_fusion.5 = bf16[2,512,512]{2,1,0:T(8,128)(2,1)} fusion(f32[512,512]{1,0:T(8,128)S(1)} %get-tuple-element.33, f32[2,512,512]{2,1,0:T(8,128)} %copy-done.2, f32[2,512,512]{2,1,0:T(8,128)S(1)} %fusion.2, f32[2,512,512]{2,1,0:T(8,128)} %copy-done.6, f32[2]{0:T(128)S(1)} %get-tuple-element.29, f32[512,512]{1,0:T(8,128)} %copy-done.7), kind=kOutput, calls=%fused_computation.15 | convolution fusion | flops 1080557568 | bytes 9437192 | tf_op jit(solution)/shard_map/cond/branch_1_fun/kij,kjl->kil/dot_general | solution.py:15
  215.0 1.7 convolution_convert_fusion.4
  216.7 4.2 %fusion.3 = f32[2,512,512]{2,1,0:T(8,128)} fusion(bf16[2,512,512]{2,1,0:T(8,128)(2,1)} %convolution_convert_fusion.4, f32[2,512,512]{2,1,0:T(8,128)S(1)} %fusion.2), kind=kOutput, calls=%fused_computation.23 | convolution fusion | flops 1074790400 | bytes 5242880 | tf_op jit(solution)/shard_map/cond/branch_1_fun/kij,kjl->kil/dot_general | solution.py:15
  220.9 4.1 %convolution_convert_fusion.1 = bf16[2,512,512]{2,1,0:T(8,128)(2,1)} fusion(f32[2,512,512]{2,1,0:T(8,128)} %fusion.3, f32[512,512]{1,0:T(8,128)S(1)} %get-tuple-element.33), kind=kOutput, calls=%fused_computation.11 | convolution fusion | flops 538968064 | bytes 4194304 | tf_op jit(solution)/shard_map/cond/branch_1_fun/kij,kjl->kil/dot_general | solution.py:15
  225.0 3.8 %multiply_convert_fusion.1 = bf16[2,512,512]{2,1,0:T(8,128)(2,1)} fusion(bf16[2,512,512]{2,1,0:T(8,128)(2,1)} %convolution_convert_fusion.1, f32[2,512,512]{2,1,0:T(8,128)S(1)} %copy-done.1, f32[512,512]{1,0:T(8,128)S(1)} %get-tuple-element.33), kind=kOutput, calls=%fused_computation.3 | convolution fusion | flops 1076363264 | bytes 5242880 | tf_op jit(solution)/shard_map/cond/branch_1_fun/kij,kjl->kil/dot_general | solution.py:15
  228.8 3.9 %multiply_convert_fusion = bf16[2,512,512]{2,1,0:T(8,128)(2,1)} fusion(bf16[2,512,512]{2,1,0:T(8,128)(2,1)} %multiply_convert_fusion.1, bf16[2,512,512]{2,1,0:T(8,128)(2,1)} %convolution_convert_fusion.5, f32[2]{0:T(128)S(1)} %get-tuple-element.28, f32[2,512,512]{2,1,0:T(8,128)S(1)} %copy-done.1, f32[512,512]{1,0:T(8,128)S(1)} %get-tuple-element.33), kind=kOutput, calls=%fused_computation.2 | convolution fusion | flops 1076887552 | bytes 6291464 | tf_op jit(solution)/shard_map/cond/branch_1_fun/kij,kjl->kil/dot_general | solution.py:15
  232.6 2.9 %multiply_reduce_fusion.1 = (f32[]{:T(128)}, f32[512,512]{1,0:T(8,128)S(1)}) fusion(bf16[2,512,512]{2,1,0:T(8,128)(2,1)} %multiply_convert_fusion, bf16[512,512]{1,0:T(8,128)(2,1)} %bitcast.64), kind=kOutput, calls=%fused_computation.29 | convolution fusion | flops 537657344 | bytes 2621444 | tf_op jit(solution)/shard_map/cond/branch_1_fun/dot_general | solution.py:53
  238.8 18.3 %all_to_all.14 = bf16[1,8,64,512]{3,2,0,1:T(8,128)(2,1)S(1)} all-to-all(bf16[1,8,64,512]{3,2,0,1:T(8,128)(2,1)} %bitcast.16), channel_id=1, replica_groups=mesh['dp'=8,'mp'=4] {'dp'}, dimensions={1} | all-to-all | bytes 1048576 | tf_op jit(solution)/shard_map/all_to_all | solution.py:102
  (30 shorter events, 7.1 us)
Async XLA Ops:
  7.2 7.7 %copy-start = (bf16[256,512]{1,0:T(8,128)(2,1)S(1)}, bf16[256,512]{1,0:T(8,128)(2,1)}, u32[]{:S(2)}) copy-start(bf16[256,512]{1,0:T(8,128)(2,1)} %param.7) | copy-start | bytes 786436
  7.2 164.1 %reduce-scatter.2.cloned.1.call-start = ((), (), s32[]{:S(2)}) async-start(), calls=%async_computation.3 | async-start | bytes 9437184 | tf_op jit(solution)/shard_map/reduce_scatter | solution.py:80
  7.2 3.2 %copy-start.8 = (bf16[256,4096]{1,0:T(8,128)(2,1)S(1)}, bf16[256,4096]{1,0:T(8,128)(2,1)}, u32[]{:S(2)}) copy-start(bf16[256,4096]{1,0:T(8,128)(2,1)} %param.6) | copy-start | bytes 6291460
  20.9 150.4 %copy-start.9 = (s32[8]{0:T(128)S(1)}, s32[8]{0:T(128)}, u32[]{:S(2)}) copy-start(s32[8]{0:T(128)} %param.9) | copy-start | bytes 100
  173.7 18.4 %all-to-all-start = ((bf16[8,1,64,512]{3,2,1,0:T(8,128)(2,1)}), bf16[8,1,64,512]{3,2,1,0:T(8,128)(2,1)S(1)}, u32[]{:S(2)}, u32[]{:S(2)}) async-start(bf16[8,1,64,512]{3,2,1,0:T(8,128)(2,1)} %copy.12), calls=%async_computation.1 | async-start | bytes 1048576 | tf_op jit(solution)/shard_map/all_to_all | solution.py:92
  192.1 0.8 copy-start.3
  192.2 3.9 %copy-start.7 = (f32[512,512]{1,0:T(8,128)}, f32[512,512]{1,0:T(8,128)S(1)}, u32[]{:S(2)}) copy-start(f32[512,512]{1,0:T(8,128)S(1)} %get-tuple-element.32) | copy-start | bytes 3145732 | tf_op jit(solution)/shard_map/cond
  192.9 1.6 copy-start.5
  196.1 1.3 copy-start.6
  203.4 1.4 copy-start.2
  220.9 4.1 %copy-start.1 = (f32[2,512,512]{2,1,0:T(8,128)S(1)}, f32[2,512,512]{2,1,0:T(8,128)}, u32[]{:S(2)}) copy-start(f32[2,512,512]{2,1,0:T(8,128)} %fusion.3) | copy-start | bytes 6291460 | tf_op jit(solution)/shard_map/cond
  232.6 3.6 %copy-start.4 = (bf16[8,1,64,512]{3,2,1,0:T(8,128)(2,1)S(1)}, bf16[8,1,64,512]{3,2,1,0:T(8,128)(2,1)}, u32[]{:S(2)}) copy-start(bf16[8,1,64,512]{3,2,1,0:T(8,128)(2,1)} %copy-done.3) | copy-start | bytes 1572868 | tf_op jit(solution)/shard_map/cond
Sparse Core Ops, SparseCore 0:
  21.1 150.1 reduce-scatter.1
where the time goes:
time: 266 us; the launch traced here: 265 us
  waiting for transfers between devices  164 us (62%)
  matrix products  45.7 us (17%)
  blocking collectives  18.3 us (7%)
  between operations  14.8 us (6%)
  local copies, waits for them, and re-layouts  13.5 us (5%)
  other arithmetic  4.26 us (2%)
  starting transfers between devices  3.75 us (1%)
    reduce_scatter x1, waiting for transfers between devices, on_device(): lax.psum_scatter(jnp.einsum('twr,tc->rwc', split_acts, cotangent, preferr...  150 us
    dot_general x10, matrix products, batched(): jnp.einsum('kij,kjl->kil', former.astype(jnp.bfloat16), latter.astype(jnp...  33.9 us
    all_to_all x1, blocking collectives, on_device(): lax.all_to_all(outgoing_rows, 'dp', split_axis=1, concat_axis=1, tiled=True)  18.3 us
    all_to_all x1, waiting for transfers between devices, on_device(): lax.all_to_all(outgoing, 'dp', split_axis=0, concat_axis=2, tiled=True)  13.2 us
    dot_general x1, matrix products, on_device(): jnp.einsum('twr,tc->rwc', split_acts, cotangent, preferred_element_type=j...  6.07 us
  transfers between devices with their start and end apart: 2, of which 2 were waited for; matrix products, arithmetic and copies ran while one was open for 0% of the time, Pallas kernels for 0%

commit v1 on v0

--- a/solution.py
+++ b/solution.py
@@ -1,6 +1,8 @@
 import jax
 import jax.numpy as jnp
 from jax import lax
+from jax.experimental import pallas as pl
+from jax.experimental.pallas import tpu as pltpu
 from jax.sharding import PartitionSpec as P
 
 ITERS = 5
@@ -111,9 +113,315 @@
     return (result, new_stats)
 
 
+MESH = pl.DeviceIdType.MESH
+LANES = 2
+CHUNKS = 2
+
+
+def gather_kernel(block_ref, acts_ref, cot_ref, grad_ref, stage, acts_all, cot_all, total,
+                  a_send, a_recv, sib_send, sib_recv, y_send, y_recv, fwd_send, fwd_recv,
+                  own_send, z_send, x_send, c_recv, load_sem, quarters, wholes):
+    dp_count, tokens, blk = acts_all.shape
+    mp_count = lax.axis_size("mp")
+    part = tokens // mp_count
+    chunk = tokens // CHUNKS
+    depth = dp_count // LANES
+    me = lax.axis_index("dp")
+    mine = lax.axis_index("mp")
+    z, x = me // LANES, me % LANES
+    sibling = mine + 1 - 2 * (mine % 2)
+    beside = (mine + 2) % mp_count
+    my_rows = pl.ds(pl.multiple_of(mine * part, part), part)
+    beside_rows = pl.ds(pl.multiple_of(beside * part, part), part)
+    others = [(me + step) % dp_count for step in range(1, dp_count)]
+    greeted = [(d, mine) for d in others] + [(me, sibling), (me, beside)]
+
+    barrier = pltpu.get_barrier_semaphore()
+    for d, m in greeted:
+        pl.semaphore_signal(barrier, inc=1, device_id={"dp": d, "mp": m}, device_id_type=MESH)
+
+    quarter_loads, whole_loads = [], []
+    for w in range(dp_count):
+        cols = pl.ds(w * blk, blk)
+        quarter_loads.append(pltpu.make_async_copy(acts_ref.at[my_rows, cols], quarters.at[w], load_sem.at[0, w]))
+        whole_loads.append(pltpu.make_async_copy(acts_ref.at[:, cols], wholes.at[w], load_sem.at[1, w]))
+    for load in quarter_loads + whole_loads:
+        load.start()
+    for load in quarter_loads:
+        load.wait()
+    for d in range(dp_count):
+        stage[d] = quarters[block_ref[d]]
+    for load in whole_loads:
+        load.wait()
+    acts_all[me] = wholes[block_ref[me]]
+    pl.semaphore_wait(barrier, len(greeted))
+
+    def remote(src, dst, send, recv, d, m):
+        return pltpu.make_async_remote_copy(
+            src_ref=src, dst_ref=dst, send_sem=send, recv_sem=recv,
+            device_id={"dp": d, "mp": m}, device_id_type=MESH)
+
+    def acts_out(d):
+        return remote(stage.at[d], acts_all.at[me, my_rows], a_send.at[d], a_recv.at[me], d, mine)
+
+    def arrived(ref, sem):
+        pltpu.make_async_copy(ref, ref, sem).wait()
+
+    def rows_of(c):
+        return pl.ds(c * chunk, chunk)
+
+    def cot_piece(who, c):
+        return cot_all.at[who, rows_of(c)]
+
+    def own_out(way, c):
+        target = (me + 1 - 2 * x, me + LANES, me - LANES)[way]
+        return remote(cot_ref.at[rows_of(c)], cot_piece(me, c), own_send.at[way, c],
+                      c_recv.at[me, c], target, mine)
+
+    def z_out(zz, sign, c):
+        who = zz * LANES + x
+        return remote(cot_piece(who, c), cot_piece(who, c), z_send.at[zz, c], c_recv.at[who, c],
+                      me + sign * LANES, mine)
+
+    def x_out(zz, c):
+        who = zz * LANES + x
+        return remote(cot_piece(who, c), cot_piece(who, c), x_send.at[zz, c], c_recv.at[who, c],
+                      me + 1 - 2 * x, mine)
+
+    def side_out(s, which):
+        if which == 0:
+            return remote(acts_all.at[s, my_rows], acts_all.at[s, my_rows], sib_send.at[s],
+                          sib_recv.at[s], me, sibling)
+        if which == 1:
+            return remote(acts_all.at[s, my_rows], acts_all.at[s, my_rows], y_send.at[s],
+                          y_recv.at[s], me, beside)
+        return remote(acts_all.at[s, beside_rows], acts_all.at[s, beside_rows], fwd_send.at[s],
+                      fwd_recv.at[s], me, sibling)
+
+    far_first = sorted(range(1, dp_count), key=lambda step: -min(step, dp_count - step))
+    ordered = [(me + step) % dp_count for step in far_first]
+    senders = [(me + dp_count - step) % dp_count for step in far_first]
+
+    def own_everywhere(act):
+        for c in range(CHUNKS):
+            pl.when(z + 1 < depth)(lambda c=c: act(own_out(1, c)))
+            pl.when(z > 0)(lambda c=c: act(own_out(2, c)))
+            act(own_out(0, c))
+
+    own_everywhere(lambda copy: copy.start())
+    for d in ordered:
+        acts_out(d).start()
+
+    def relay(zz, sign, c):
+        who = zz * LANES + x
+        arrived(cot_piece(who, c), c_recv.at[who, c])
+        nxt = z + sign
+        pl.when(jnp.logical_and(nxt >= 0, nxt < depth))(lambda: z_out(zz, sign, c).start())
+        x_out(zz, c).start()
+
+    def relays(k):
+        for c in range(CHUNKS):
+            pl.when(z - k >= 0)(lambda c=c: relay(z - k, 1, c))
+            pl.when(z + k < depth)(lambda c=c: relay(z + k, -1, c))
+
+    def add_term(s, cot, first=False):
+        term = lax.dot_general(acts_all[s], cot, (((0,), (0,)), ((), ())),
+                               preferred_element_type=jnp.float32)
+        total[...] = term if first else total[...] + term
+
+    add_term(me, cot_ref[...], True)
+    relays(1)
+    for s in senders:
+        arrived(acts_all.at[s, my_rows], a_recv.at[s])
+        side_out(s, 0).start()
+        side_out(s, 1).start()
+    for k in range(2, depth):
+        relays(k)
+    for s in senders:
+        arrived(acts_all.at[s, beside_rows], y_recv.at[s])
+        side_out(s, 2).start()
+    across = beside + 1 - 2 * (beside % 2)
+    sibling_rows = pl.ds(pl.multiple_of(sibling * part, part), part)
+    across_rows = pl.ds(pl.multiple_of(across * part, part), part)
+
+    def acts_ready(s):
+        arrived(acts_all.at[s, sibling_rows], sib_recv.at[s])
+        arrived(acts_all.at[s, across_rows], fwd_recv.at[s])
+
+    for k in range(1, depth):
+        s = ((z + k) % depth) * LANES + x
+        acts_ready(s)
+        add_term(s, cot_all[s])
+    for k in range(depth):
+        s = ((z + k) % depth) * LANES + 1 - x
+        acts_ready(s)
+        for c in range(CHUNKS):
+            arrived(cot_piece(s, c), c_recv.at[s, c])
+        add_term(s, cot_all[s])
+    grad_ref[...] = total[...].astype(grad_ref.dtype)
+
+    own_everywhere(lambda copy: copy.wait_send())
+    for d in ordered:
+        acts_out(d).wait_send()
+    for s in senders:
+        for which in range(3):
+            side_out(s, which).wait_send()
+
+    def relay_sent(zz, sign, c):
+        nxt = z + sign
+        pl.when(jnp.logical_and(nxt >= 0, nxt < depth))(lambda: z_out(zz, sign, c).wait_send())
+        x_out(zz, c).wait_send()
+
+    for k in range(1, depth):
+        for c in range(CHUNKS):
+            pl.when(z - k >= 0)(lambda c=c, k=k: relay_sent(z - k, 1, c))
+            pl.when(z + k < depth)(lambda c=c, k=k: relay_sent(z + k, -1, c))
+
+
+def gather_gradient(slot_block, acts, cotangent, dp_count, mp_count):
+    tokens, blk = cotangent.shape
+    dma = pltpu.SemaphoreType.DMA
+    depth = dp_count // LANES
+    vmem = pl.BlockSpec(memory_space=pltpu.VMEM)
+    return pl.pallas_call(
+        gather_kernel,
+        name="gather_gradient",
+        out_shape=jax.ShapeDtypeStruct((blk, blk), jnp.bfloat16),
+        in_specs=[pl.BlockSpec(memory_space=pltpu.SMEM), pl.BlockSpec(memory_space=pl.ANY), vmem],
+        out_specs=vmem,
+        scratch_shapes=[
+            pltpu.VMEM((dp_count, tokens // mp_count, blk), jnp.bfloat16),
+            pltpu.VMEM((dp_count, tokens, blk), jnp.bfloat16),
+            pltpu.VMEM((dp_count, tokens, blk), jnp.bfloat16),
+            pltpu.VMEM((blk, blk), jnp.float32),
+        ] + [dma((dp_count,))] * 8 + [dma((3, CHUNKS)), dma((depth, CHUNKS)), dma((depth, CHUNKS)),
+                                     dma((dp_count, CHUNKS)), dma((2, dp_count)),
+                                     pltpu.VMEM((dp_count, tokens // mp_count, blk), jnp.bfloat16),
+                                     pltpu.VMEM((dp_count, tokens, blk), jnp.bfloat16)],
+        compiler_params=pltpu.CompilerParams(collective_id=0, has_side_effects=True),
+    )(slot_block, acts, cotangent)
+
+
+def mm(former, latter):
+    return jnp.dot(former, latter, preferred_element_type=jnp.float32)
+
+
+def root_kernel(grad_ref, stat_ref, dir_ref, new_ref):
+    low = jnp.bfloat16
+    blk = grad_ref.shape[0]
+    grad = grad_ref[...]
+    row = lax.broadcasted_iota(jnp.int32, (blk, blk), 0)
+    col = lax.broadcasted_iota(jnp.int32, (blk, blk), 1)
+    diagonal = row == col
+    grams = [
+        lax.dot_general(grad, grad, (((1,), (1,)), ((), ())), preferred_element_type=jnp.float32),
+        lax.dot_general(grad, grad, (((0,), (0,)), ((), ())), preferred_element_type=jnp.float32),
+    ]
+    moments, results, scales = [], [None, None], []
+    for side in range(2):
+        fresh = BETA * stat_ref[side] + (1.0 - BETA) * grams[side]
+        new_ref[side] = fresh
+        damped = fresh + jnp.where(diagonal, DAMPING, 0.0)
+        frob = jnp.sqrt(jnp.sum(damped * damped, axis=(0, 1), keepdims=True) + EPSILON)
+        scales.append(lax.rsqrt(jnp.sqrt(frob)))
+        moments.append(damped * (1.0 / frob))
+    for iteration in range(ITERS):
+        factors = [(jnp.where(diagonal, 5.0, 0.0) - moments[side]) * 0.25 for side in range(2)]
+        lows = [factors[side].astype(low) for side in range(2)]
+        if iteration + 1 < ITERS:
+            squares = [mm(lows[side], lows[side]).astype(low) for side in range(2)]
+            inner = [mm(squares[side], moments[side].astype(low)).astype(low) for side in range(2)]
+            moments = [mm(squares[side], inner[side]) for side in range(2)]
+        for side in range(2):
+            results[side] = factors[side] if iteration == 0 else mm(results[side].astype(low), lows[side])
+    roots = [(results[side] * scales[side]).astype(low) for side in range(2)]
+    direction = mm(mm(roots[0], grad).astype(low), roots[1])
+    wide = grad.astype(jnp.float32)
+    count = blk * blk
+    power = jnp.sum(wide * wide, axis=(0, 1), keepdims=True) / count + EPSILON
+    reached = jnp.sum(direction * direction, axis=(0, 1), keepdims=True) / count + EPSILON
+    dir_ref[...] = (direction * jnp.sqrt(power / reached)).astype(low)
+
+
+def apply_roots(grad, stat_pair):
+    vmem = pl.BlockSpec(memory_space=pltpu.VMEM)
+    return pl.pallas_call(
+        root_kernel,
+        name="apply_roots",
+        out_shape=(jax.ShapeDtypeStruct(grad.shape, jnp.bfloat16),
+                   jax.ShapeDtypeStruct(stat_pair.shape, jnp.float32)),
+        in_specs=[vmem, vmem],
+        out_specs=(vmem, vmem),
+    )(grad, stat_pair)
+
+
+def return_kernel(owner_ref, dir_ref, out_ref, held, send, recv):
+    dp_count, piece, blk = held.shape
+    me = lax.axis_index("dp")
+    others = [(me + step) % dp_count for step in range(1, dp_count)]
+    barrier = pltpu.get_barrier_semaphore()
+    for d in others:
+        pl.semaphore_signal(barrier, inc=1, device_id={"dp": d}, device_id_type=MESH)
+    pl.semaphore_wait(barrier, len(others))
+
+    def rows_of(d):
+        return pl.ds(pl.multiple_of(d * piece, piece), piece)
+
+    far_first = sorted(range(1, dp_count), key=lambda step: -min(step, dp_count - step))
+    copies = []
+    for step in far_first:
+        d = (me + step) % dp_count
+        copy = pltpu.make_async_remote_copy(
+            src_ref=dir_ref.at[rows_of(d)], dst_ref=held.at[me], send_sem=send.at[d],
+            recv_sem=recv.at[me], device_id={"dp": d}, device_id_type=MESH)
+        copy.start()
+        copies.append(copy)
+    held[me] = dir_ref[rows_of(me)]
+    for d in others:
+        pltpu.make_async_copy(held.at[d], held.at[d], recv.at[d]).wait()
+    for w in range(dp_count):
+        out_ref[w] = held[owner_ref[w]]
+    for copy in copies:
+        copy.wait_send()
+
+
+def return_rows(owner_slot, direction, dp_count):
+    blk = direction.shape[0]
+    shape = (dp_count, blk // dp_count, blk)
+    vmem = pl.BlockSpec(memory_space=pltpu.VMEM)
+    dma = pltpu.SemaphoreType.DMA
+    return pl.pallas_call(
+        return_kernel,
+        name="return_rows",
+        out_shape=jax.ShapeDtypeStruct(shape, jnp.bfloat16),
+        in_specs=[pl.BlockSpec(memory_space=pltpu.SMEM), vmem],
+        out_specs=vmem,
+        scratch_shapes=[pltpu.VMEM(shape, jnp.bfloat16), dma((dp_count,)), dma((dp_count,))],
+        compiler_params=pltpu.CompilerParams(collective_id=1, has_side_effects=True),
+    )(owner_slot, direction)
+
+
+def full_house(acts, cotangent, stats, owner_slot):
+    dp_count, mp_count = lax.axis_size("dp"), lax.axis_size("mp")
+    ids = jnp.arange(dp_count, dtype=jnp.int32)
+    slot_block = jnp.sum(jnp.where(owner_slot[None, :] == ids[:, None], ids[None, :], 0), axis=1)
+    grad = gather_gradient(slot_block, acts, cotangent, dp_count, mp_count)
+    direction, new_pair = apply_roots(grad, stats[0, 0])
+    return return_rows(owner_slot, direction, dp_count), new_pair[None, None]
+
+
+def device_body(acts, cotangent, stats, owner_slot):
+    dp_count, mp_count = lax.axis_size("dp"), lax.axis_size("mp")
+    blk = cotangent.shape[1]
+    every_slot_filled = stats.shape[1] == 1 and acts.shape[1] == dp_count * blk
+    if every_slot_filled and mp_count == 4 and dp_count % LANES == 0 and dp_count <= 8:
+        return full_house(acts, cotangent, stats, owner_slot)
+    return on_device(acts, cotangent, stats, owner_slot)
+
+
 def solution(mesh):
     return jax.shard_map(
-        on_device,
+        device_body,
         mesh=mesh,
         in_specs=(P("dp", None), P("dp", "mp"), P("mp", "dp", None, None, None), P()),
         out_specs=(P(None, "dp", "mp"), P("mp", "dp", None, None, None)),

time: 266 us -> 74.8 us (0.28)
  waiting for transfers between devices: 164 us -> 0 us
  Pallas kernels: 0 us -> 70.8 us
  matrix products: 45.7 us -> 0 us
  blocking collectives: 18.3 us -> 0 us
  between operations: 14.8 us -> 0.65 us
  local copies, waits for them, and re-layouts: 13.5 us -> 1.87 us
  starting transfers between devices: 3.75 us -> 0 us
  other arithmetic: 4.26 us -> 1.28 us
    reduce_scatter x1 -> x0, waiting for transfers between devices: 150 us -> none  [on_device(): lax.psum_scatter(jnp.einsum('twr,tc->rwc', split_acts, cotangent, preferr...]
    pallas_call x0 -> x3, Pallas kernels: none -> 70.8 us  [the longest x1 42 us: gather_gradient(): pl.pallas_call(gather_kernel, name='gather_gradient', out_shape=jax.Shape...]
    dot_general x16 -> x0, matrix products: 45.7 us -> none  [the longest x10 33.9 us: batched(): jnp.einsum('kij,kjl->kil', former.astype(jnp.bfloat16), latter.astype(jnp...]
    all_to_all x1 -> x0, blocking collectives: 18.3 us -> none  [on_device(): lax.all_to_all(outgoing_rows, 'dp', split_axis=1, concat_axis=1, tiled=True)]
    all_to_all x1 -> x0, waiting for transfers between devices: 13.2 us -> none  [on_device(): lax.all_to_all(outgoing, 'dp', split_axis=0, concat_axis=2, tiled=True)]
    reshape x2 -> x0, local copies, waits for them, and re-layouts: 4.43 us -> none  [the longest x1 3.48 us: on_device(): split_acts = acts.reshape(acts.shape[0], blocks, blk_size)]
    cond x14 -> x0, local copies, waits for them, and re-layouts: 3.94 us -> none
    all_to_all x1 -> x0, starting transfers between devices: 3.72 us -> none  [on_device(): lax.all_to_all(outgoing, 'dp', split_axis=0, concat_axis=2, tiled=True)]
  transfers between devices with their start and end apart: 2 -> 0, of which waited for: 2 -> 0; matrix products, arithmetic and copies ran while one was open for 0% -> 0% of each run, Pallas kernels for 0% -> 0%
where the time goes in v1:
time: 74.8 us; the launch traced here: 74.6 us
  Pallas kernels  70.8 us (95%)
  local copies, waits for them, and re-layouts  1.87 us (2%)
  other arithmetic  1.28 us (2%)
    pallas_call x1, Pallas kernels, gather_gradient(): pl.pallas_call(gather_kernel, name='gather_gradient', out_shape=jax.Shape...  42 us
    pallas_call x1, Pallas kernels, return_rows(): pl.pallas_call(return_kernel, name='return_rows', out_shape=jax.ShapeDtyp...  15.2 us
    pallas_call x1, Pallas kernels, apply_roots(): pl.pallas_call(root_kernel, name='apply_roots', out_shape=(jax.ShapeDtype...  13.6 us
    unnamed x1, local copies, waits for them, and re-layouts  1.87 us

profile of v1, /device:TPU:0, one launch (start us, length us, event | category | flops | bytes accessed | tf_op | source)
XLA Modules:
  0.0 74.6 jit_solution(170046323263222442)
XLA Ops:
  0.6 1.3 %select_reduce_fusion.block_ref = s32[8]{0:T(128)} fusion(s32[8]{0:T(128)} %owner_ref.1), kind=kLoop, calls=%fused_computation | loop fusion | flops 184 | bytes 64 | tf_op jit(solution)/shard_map/reduce_sum | solution.py:407
  1.9 42.0 %gather_gradient.1.grad_ref = bf16[512,512]{1,0:T(8,128)(2,1)} custom-call(s32[8]{0:T(128)} %select_reduce_fusion.block_ref, bf16[256,4096]{1,0:T(8,128)(2,1)} %acts_ref.1, bf16[256,512]{1,0:T(8,128)(2,1)} %cot_ref.1), custom_call_target="tpu_custom_call" | custom-call | tf_op jit(solution)/shard_map/gather_gradient/pallas_call | solution.py:286
  43.9 13.6 %apply_roots.1 = (bf16[512,512]{1,0:T(8,128)(2,1)}, f32[2,512,512]{2,1,0:T(8,128)}) custom-call(bf16[512,512]{1,0:T(8,128)(2,1)} %gather_gradient.1.grad_ref, f32[2,512,512]{2,1,0:T(8,128)} %bitcast.2), custom_call_target="tpu_custom_call" | custom-call | tf_op jit(solution)/shard_map/apply_roots/pallas_call | solution.py:348
  57.5 15.2 %return_rows.1 = bf16[8,64,512]{2,1,0:T(8,128)(2,1)} custom-call(s32[8]{0:T(128)} %owner_ref.1, bf16[512,512]{1,0:T(8,128)(2,1)} %get-tuple-element.4.dir_ref), custom_call_target="tpu_custom_call" | custom-call | tf_op jit(solution)/shard_map/return_rows/pallas_call | solution.py:393
  72.7 1.9 %copy.7 = bf16[8,64,512]{2,1,0:T(8,128)(2,1)} copy(bf16[8,64,512]{2,1,0:T(8,128)(2,1)} %return_rows.1) | data formatting | bytes 1048576

commit v2 on v1

--- a/solution.py
+++ b/solution.py
@@ -115,10 +115,10 @@
 
 MESH = pl.DeviceIdType.MESH
 LANES = 2
-CHUNKS = 2
-
-
-def gather_kernel(block_ref, acts_ref, cot_ref, grad_ref, stage, acts_all, cot_all, total,
+CHUNKS = 4
+
+
+def gather_kernel(owner_ref, acts_ref, cot_ref, grad_ref, stage, acts_all, cot_all, total,
                   a_send, a_recv, sib_send, sib_recv, y_send, y_recv, fwd_send, fwd_recv,
                   own_send, z_send, x_send, c_recv, load_sem, quarters, wholes):
     dp_count, tokens, blk = acts_all.shape
@@ -136,10 +136,6 @@
     others = [(me + step) % dp_count for step in range(1, dp_count)]
     greeted = [(d, mine) for d in others] + [(me, sibling), (me, beside)]
 
-    barrier = pltpu.get_barrier_semaphore()
-    for d, m in greeted:
-        pl.semaphore_signal(barrier, inc=1, device_id={"dp": d, "mp": m}, device_id_type=MESH)
-
     quarter_loads, whole_loads = [], []
     for w in range(dp_count):
         cols = pl.ds(w * blk, blk)
@@ -147,14 +143,9 @@
         whole_loads.append(pltpu.make_async_copy(acts_ref.at[:, cols], wholes.at[w], load_sem.at[1, w]))
     for load in quarter_loads + whole_loads:
         load.start()
-    for load in quarter_loads:
-        load.wait()
-    for d in range(dp_count):
-        stage[d] = quarters[block_ref[d]]
-    for load in whole_loads:
-        load.wait()
-    acts_all[me] = wholes[block_ref[me]]
-    pl.semaphore_wait(barrier, len(greeted))
+    barrier = pltpu.get_barrier_semaphore()
+    for d, m in greeted:
+        pl.semaphore_signal(barrier, inc=1, device_id={"dp": d, "mp": m}, device_id_type=MESH)
 
     def remote(src, dst, send, recv, d, m):
         return pltpu.make_async_remote_copy(
@@ -208,9 +199,23 @@
             pl.when(z > 0)(lambda c=c: act(own_out(2, c)))
             act(own_out(0, c))
 
+    def block_at(slot):
+        found = 0
+        for w in range(1, dp_count):
+            gap = owner_ref[w] - slot
+            found = found + w * jnp.maximum(1 - gap * gap, 0)
+        return jnp.minimum(found, dp_count - 1)
+
+    pl.semaphore_wait(barrier, len(greeted))
     own_everywhere(lambda copy: copy.start())
-    for d in ordered:
-        acts_out(d).start()
+    for load in quarter_loads:
+        load.wait()
+    for d in range(dp_count):
+        stage[d] = quarters[block_at(d)]
+    for load in whole_loads:
+        load.wait()
+    acts_all[me] = wholes[block_at(me)]
+
 
     def relay(zz, sign, c):
         who = zz * LANES + x
@@ -229,17 +234,6 @@
                                preferred_element_type=jnp.float32)
         total[...] = term if first else total[...] + term
 
-    add_term(me, cot_ref[...], True)
-    relays(1)
-    for s in senders:
-        arrived(acts_all.at[s, my_rows], a_recv.at[s])
-        side_out(s, 0).start()
-        side_out(s, 1).start()
-    for k in range(2, depth):
-        relays(k)
-    for s in senders:
-        arrived(acts_all.at[s, beside_rows], y_recv.at[s])
-        side_out(s, 2).start()
     across = beside + 1 - 2 * (beside % 2)
     sibling_rows = pl.ds(pl.multiple_of(sibling * part, part), part)
     across_rows = pl.ds(pl.multiple_of(across * part, part), part)
@@ -248,16 +242,38 @@
         arrived(acts_all.at[s, sibling_rows], sib_recv.at[s])
         arrived(acts_all.at[s, across_rows], fwd_recv.at[s])
 
+    add_term(me, cot_ref[...], True)
     for k in range(1, depth):
-        s = ((z + k) % depth) * LANES + x
-        acts_ready(s)
-        add_term(s, cot_all[s])
-    for k in range(depth):
-        s = ((z + k) % depth) * LANES + 1 - x
-        acts_ready(s)
-        for c in range(CHUNKS):
-            arrived(cot_piece(s, c), c_recv.at[s, c])
-        add_term(s, cot_all[s])
+        relays(k)
+        if k == max(depth - 2, 1):
+            for d in ordered:
+                acts_out(d).start()
+
+    inward = 1 - 2 * (2 * z // depth)
+    arrivals = [(True, z * LANES + 1 - x)]
+    for k in range(1, depth):
+        zz = (z + inward * k + depth) % depth
+        arrivals += [(False, zz * LANES + x), (True, zz * LANES + 1 - x)]
+    for i in range(len(arrivals) + 2):
+        if i < len(arrivals):
+            s = arrivals[i][1]
+            arrived(acts_all.at[s, my_rows], a_recv.at[s])
+            side_out(s, 0).start()
+            side_out(s, 1).start()
+        if 1 <= i <= len(arrivals):
+            s = arrivals[i - 1][1]
+            arrived(acts_all.at[s, beside_rows], y_recv.at[s])
+            side_out(s, 2).start()
+        if i >= 2 and not arrivals[i - 2][0]:
+            s = arrivals[i - 2][1]
+            acts_ready(s)
+            add_term(s, cot_all[s])
+    for is_beside, s in arrivals:
+        if is_beside:
+            acts_ready(s)
+            for c in range(CHUNKS):
+                arrived(cot_piece(s, c), c_recv.at[s, c])
+            add_term(s, cot_all[s])
     grad_ref[...] = total[...].astype(grad_ref.dtype)
 
     own_everywhere(lambda copy: copy.wait_send())
@@ -278,7 +294,7 @@
             pl.when(z + k < depth)(lambda c=c, k=k: relay_sent(z + k, -1, c))
 
 
-def gather_gradient(slot_block, acts, cotangent, dp_count, mp_count):
+def gather_gradient(owner_slot, acts, cotangent, dp_count, mp_count):
     tokens, blk = cotangent.shape
     dma = pltpu.SemaphoreType.DMA
     depth = dp_count // LANES
@@ -299,16 +315,20 @@
                                      pltpu.VMEM((dp_count, tokens // mp_count, blk), jnp.bfloat16),
                                      pltpu.VMEM((dp_count, tokens, blk), jnp.bfloat16)],
         compiler_params=pltpu.CompilerParams(collective_id=0, has_side_effects=True),
-    )(slot_block, acts, cotangent)
+    )(owner_slot, acts, cotangent)
 
 
 def mm(former, latter):
     return jnp.dot(former, latter, preferred_element_type=jnp.float32)
 
 
-def root_kernel(grad_ref, stat_ref, dir_ref, new_ref):
+def root_kernel(grad_ref, stat_any, dir_ref, new_any, stat_ref, new_ref, in_sem, out_sem):
     low = jnp.bfloat16
     blk = grad_ref.shape[0]
+    loads = [pltpu.make_async_copy(stat_any.at[k], stat_ref.at[k], in_sem.at[k]) for k in range(2)]
+    stores = [pltpu.make_async_copy(new_ref.at[k], new_any.at[k], out_sem.at[k]) for k in range(2)]
+    for load in loads:
+        load.start()
     grad = grad_ref[...]
     row = lax.broadcasted_iota(jnp.int32, (blk, blk), 0)
     col = lax.broadcasted_iota(jnp.int32, (blk, blk), 1)
@@ -319,8 +339,10 @@
     ]
     moments, results, scales = [], [None, None], []
     for side in range(2):
+        loads[side].wait()
         fresh = BETA * stat_ref[side] + (1.0 - BETA) * grams[side]
         new_ref[side] = fresh
+        stores[side].start()
         damped = fresh + jnp.where(diagonal, DAMPING, 0.0)
         frob = jnp.sqrt(jnp.sum(damped * damped, axis=(0, 1), keepdims=True) + EPSILON)
         scales.append(lax.rsqrt(jnp.sqrt(frob)))
@@ -341,6 +363,8 @@
     power = jnp.sum(wide * wide, axis=(0, 1), keepdims=True) / count + EPSILON
     reached = jnp.sum(direction * direction, axis=(0, 1), keepdims=True) / count + EPSILON
     dir_ref[...] = (direction * jnp.sqrt(power / reached)).astype(low)
+    for store in stores:
+        store.wait()
 
 
 def apply_roots(grad, stat_pair):
@@ -350,8 +374,10 @@
         name="apply_roots",
         out_shape=(jax.ShapeDtypeStruct(grad.shape, jnp.bfloat16),
                    jax.ShapeDtypeStruct(stat_pair.shape, jnp.float32)),
-        in_specs=[vmem, vmem],
-        out_specs=(vmem, vmem),
+        in_specs=[vmem, pl.BlockSpec(memory_space=pl.ANY)],
+        out_specs=(vmem, pl.BlockSpec(memory_space=pl.ANY)),
+        scratch_shapes=[pltpu.VMEM(stat_pair.shape, jnp.float32)] * 2
+        + [pltpu.SemaphoreType.DMA((2,))] * 2,
     )(grad, stat_pair)
 
 
@@ -403,9 +429,7 @@
 
 def full_house(acts, cotangent, stats, owner_slot):
     dp_count, mp_count = lax.axis_size("dp"), lax.axis_size("mp")
-    ids = jnp.arange(dp_count, dtype=jnp.int32)
-    slot_block = jnp.sum(jnp.where(owner_slot[None, :] == ids[:, None], ids[None, :], 0), axis=1)
-    grad = gather_gradient(slot_block, acts, cotangent, dp_count, mp_count)
+    grad = gather_gradient(owner_slot, acts, cotangent, dp_count, mp_count)
     direction, new_pair = apply_roots(grad, stats[0, 0])
     return return_rows(owner_slot, direction, dp_count), new_pair[None, None]
 

time: 74.8 us -> 86.3 us (1.15)
  Pallas kernels: 70.8 us -> 83.5 us
  other arithmetic: 1.28 us -> 0 us
    pallas_call x1, Pallas kernels: 42 us -> 49.2 us  [gather_gradient(): pl.pallas_call(gather_kernel, name='gather_gradient', out_shape=jax.Shape...]
    pallas_call x1, Pallas kernels: 15.2 us -> 19.9 us  [return_rows(): pl.pallas_call(return_kernel, name='return_rows', out_shape=jax.ShapeDtyp...]
    reduce_sum x1 -> x0, other arithmetic: 1.28 us -> none  [full_house(): jnp.sum(jnp.where(owner_slot[None, :] == ids[:, None], ids[None, :], 0),...]
where the time goes in v2:
time: 86.3 us; the launch traced here: 86 us
  Pallas kernels  83.5 us (97%)
  local copies, waits for them, and re-layouts  1.87 us (2%)
    pallas_call x1, Pallas kernels, gather_gradient(): pl.pallas_call(gather_kernel, name='gather_gradient', out_shape=jax.Shape...  49.2 us
    pallas_call x1, Pallas kernels, return_rows(): pl.pallas_call(return_kernel, name='return_rows', out_shape=jax.ShapeDtyp...  19.9 us
    pallas_call x1, Pallas kernels, apply_roots(): pl.pallas_call(root_kernel, name='apply_roots', out_shape=(jax.ShapeDtype...  14.3 us
    unnamed x1, local copies, waits for them, and re-layouts  1.87 us

profile of v2, /device:TPU:0, one launch (start us, length us, event | category | flops | bytes accessed | tf_op | source)
XLA Modules:
  0.0 86.0 jit_solution(11401294540229165793)
XLA Ops:
  0.6 49.2 %gather_gradient.1.grad_ref = bf16[512,512]{1,0:T(8,128)(2,1)} custom-call(s32[8]{0:T(128)} %owner_ref.3, bf16[256,4096]{1,0:T(8,128)(2,1)} %acts_ref.1, bf16[256,512]{1,0:T(8,128)(2,1)} %cot_ref.1), custom_call_target="tpu_custom_call" | custom-call | tf_op jit(solution)/shard_map/gather_gradient/pallas_call | solution.py:302
  49.9 14.3 %apply_roots.1 = (bf16[512,512]{1,0:T(8,128)(2,1)}, f32[2,512,512]{2,1,0:T(8,128)}) custom-call(bf16[512,512]{1,0:T(8,128)(2,1)} %gather_gradient.1.grad_ref, f32[2,512,512]{2,1,0:T(8,128)} %bitcast.2), custom_call_target="tpu_custom_call" | custom-call | tf_op jit(solution)/shard_map/apply_roots/pallas_call | solution.py:372
  64.2 19.9 %return_rows.1 = bf16[8,64,512]{2,1,0:T(8,128)(2,1)} custom-call(s32[8]{0:T(128)} %owner_ref.3, bf16[512,512]{1,0:T(8,128)(2,1)} %get-tuple-element.4.dir_ref), custom_call_target="tpu_custom_call" | custom-call | tf_op jit(solution)/shard_map/return_rows/pallas_call | solution.py:419
  84.1 1.9 %copy.7 = bf16[8,64,512]{2,1,0:T(8,128)(2,1)} copy(bf16[8,64,512]{2,1,0:T(8,128)(2,1)} %return_rows.1) | data formatting | bytes 1048576

commit v3 on v2

--- a/solution.py
+++ b/solution.py
@@ -115,7 +115,7 @@
 
 MESH = pl.DeviceIdType.MESH
 LANES = 2
-CHUNKS = 4
+CHUNKS = 2
 
 
 def gather_kernel(owner_ref, acts_ref, cot_ref, grad_ref, stage, acts_all, cot_all, total,
@@ -206,12 +206,19 @@
             found = found + w * jnp.maximum(1 - gap * gap, 0)
         return jnp.minimum(found, dp_count - 1)
 
-    pl.semaphore_wait(barrier, len(greeted))
-    own_everywhere(lambda copy: copy.start())
+    inward = 1 - 2 * (2 * z // depth)
+    arrivals = [(True, z * LANES + 1 - x)]
+    for k in range(1, depth):
+        zz = (z + inward * k + depth) % depth
+        arrivals += [(False, zz * LANES + x), (True, zz * LANES + 1 - x)]
     for load in quarter_loads:
         load.wait()
     for d in range(dp_count):
         stage[d] = quarters[block_at(d)]
+    pl.semaphore_wait(barrier, len(greeted))
+    own_everywhere(lambda copy: copy.start())
+    for _, d in arrivals:
+        acts_out(d).start()
     for load in whole_loads:
         load.wait()
     acts_all[me] = wholes[block_at(me)]
@@ -243,18 +250,9 @@
         arrived(acts_all.at[s, across_rows], fwd_recv.at[s])
 
     add_term(me, cot_ref[...], True)
-    for k in range(1, depth):
-        relays(k)
-        if k == max(depth - 2, 1):
-            for d in ordered:
-                acts_out(d).start()
-
-    inward = 1 - 2 * (2 * z // depth)
-    arrivals = [(True, z * LANES + 1 - x)]
-    for k in range(1, depth):
-        zz = (z + inward * k + depth) % depth
-        arrivals += [(False, zz * LANES + x), (True, zz * LANES + 1 - x)]
     for i in range(len(arrivals) + 2):
+        if i % LANES == 0 and i // LANES + 1 < depth:
+            relays(i // LANES + 1)
         if i < len(arrivals):
             s = arrivals[i][1]
             arrived(acts_all.at[s, my_rows], a_recv.at[s])
@@ -264,8 +262,8 @@
             s = arrivals[i - 1][1]
             arrived(acts_all.at[s, beside_rows], y_recv.at[s])
             side_out(s, 2).start()
-        if i >= 2 and not arrivals[i - 2][0]:
-            s = arrivals[i - 2][1]
+    for is_beside, s in arrivals:
+        if not is_beside:
             acts_ready(s)
             add_term(s, cot_all[s])
     for is_beside, s in arrivals:
@@ -322,13 +320,9 @@
     return jnp.dot(former, latter, preferred_element_type=jnp.float32)
 
 
-def root_kernel(grad_ref, stat_any, dir_ref, new_any, stat_ref, new_ref, in_sem, out_sem):
+def root_kernel(grad_ref, stat_ref, dir_ref, new_ref):
     low = jnp.bfloat16
     blk = grad_ref.shape[0]
-    loads = [pltpu.make_async_copy(stat_any.at[k], stat_ref.at[k], in_sem.at[k]) for k in range(2)]
-    stores = [pltpu.make_async_copy(new_ref.at[k], new_any.at[k], out_sem.at[k]) for k in range(2)]
-    for load in loads:
-        load.start()
     grad = grad_ref[...]
     row = lax.broadcasted_iota(jnp.int32, (blk, blk), 0)
     col = lax.broadcasted_iota(jnp.int32, (blk, blk), 1)
@@ -339,10 +333,8 @@
     ]
     moments, results, scales = [], [None, None], []
     for side in range(2):
-        loads[side].wait()
         fresh = BETA * stat_ref[side] + (1.0 - BETA) * grams[side]
         new_ref[side] = fresh
-        stores[side].start()
         damped = fresh + jnp.where(diagonal, DAMPING, 0.0)
         frob = jnp.sqrt(jnp.sum(damped * damped, axis=(0, 1), keepdims=True) + EPSILON)
         scales.append(lax.rsqrt(jnp.sqrt(frob)))
@@ -363,8 +355,6 @@
     power = jnp.sum(wide * wide, axis=(0, 1), keepdims=True) / count + EPSILON
     reached = jnp.sum(direction * direction, axis=(0, 1), keepdims=True) / count + EPSILON
     dir_ref[...] = (direction * jnp.sqrt(power / reached)).astype(low)
-    for store in stores:
-        store.wait()
 
 
 def apply_roots(grad, stat_pair):
@@ -374,10 +364,8 @@
         name="apply_roots",
         out_shape=(jax.ShapeDtypeStruct(grad.shape, jnp.bfloat16),
                    jax.ShapeDtypeStruct(stat_pair.shape, jnp.float32)),
-        in_specs=[vmem, pl.BlockSpec(memory_space=pl.ANY)],
-        out_specs=(vmem, pl.BlockSpec(memory_space=pl.ANY)),
-        scratch_shapes=[pltpu.VMEM(stat_pair.shape, jnp.float32)] * 2
-        + [pltpu.SemaphoreType.DMA((2,))] * 2,
+        in_specs=[vmem, vmem],
+        out_specs=(vmem, vmem),
     )(grad, stat_pair)
 
 

time: 86.3 us -> 77.4 us (0.90)
  Pallas kernels: 83.5 us -> 74.6 us
    pallas_call x1, Pallas kernels: 19.9 us -> 15.8 us  [return_rows(): pl.pallas_call(return_kernel, name='return_rows', out_shape=jax.ShapeDtyp...]
    pallas_call x1, Pallas kernels: 49.2 us -> 45.2 us  [gather_gradient(): pl.pallas_call(gather_kernel, name='gather_gradient', out_shape=jax.Shape...]
where the time goes in v3:
time: 77.4 us; the launch traced here: 77.1 us
  Pallas kernels  74.6 us (96%)
  local copies, waits for them, and re-layouts  1.87 us (2%)
    pallas_call x1, Pallas kernels, gather_gradient(): pl.pallas_call(gather_kernel, name='gather_gradient', out_shape=jax.Shape...  45.2 us
    pallas_call x1, Pallas kernels, return_rows(): pl.pallas_call(return_kernel, name='return_rows', out_shape=jax.ShapeDtyp...  15.8 us
    pallas_call x1, Pallas kernels, apply_roots(): pl.pallas_call(root_kernel, name='apply_roots', out_shape=(jax.ShapeDtype...  13.5 us
    unnamed x1, local copies, waits for them, and re-layouts  1.87 us

profile of v3, /device:TPU:0, one launch (start us, length us, event | category | flops | bytes accessed | tf_op | source)
XLA Modules:
  0.0 77.1 jit_solution(14437050790115630162)
XLA Ops:
  0.6 45.2 %gather_gradient.1.grad_ref = bf16[512,512]{1,0:T(8,128)(2,1)} custom-call(s32[8]{0:T(128)} %owner_ref.3, bf16[256,4096]{1,0:T(8,128)(2,1)} %acts_ref.1, bf16[256,512]{1,0:T(8,128)(2,1)} %cot_ref.1), custom_call_target="tpu_custom_call" | custom-call | tf_op jit(solution)/shard_map/gather_gradient/pallas_call | solution.py:300
  45.9 13.5 %apply_roots.1 = (bf16[512,512]{1,0:T(8,128)(2,1)}, f32[2,512,512]{2,1,0:T(8,128)}) custom-call(bf16[512,512]{1,0:T(8,128)(2,1)} %gather_gradient.1.grad_ref, f32[2,512,512]{2,1,0:T(8,128)} %bitcast.2), custom_call_target="tpu_custom_call" | custom-call | tf_op jit(solution)/shard_map/apply_roots/pallas_call | solution.py:362
  59.4 15.8 %return_rows.1 = bf16[8,64,512]{2,1,0:T(8,128)(2,1)} custom-call(s32[8]{0:T(128)} %owner_ref.3, bf16[512,512]{1,0:T(8,128)(2,1)} %get-tuple-element.4.dir_ref), custom_call_target="tpu_custom_call" | custom-call | tf_op jit(solution)/shard_map/return_rows/pallas_call | solution.py:407
  75.2 1.9 %copy.7 = bf16[8,64,512]{2,1,0:T(8,128)(2,1)} copy(bf16[8,64,512]{2,1,0:T(8,128)(2,1)} %return_rows.1) | data formatting | bytes 1048576
